TPU v7x, 256 devices: a whole 4x4x8 slice. The times are simulated.
256 devices in a mesh: slab: 128 (over z, x, y), graph: 2 (over core).
Axes of the slice: x: 4, y: 4, z: 8, core: 2. Of those that a mesh axis runs over, the one named last changes fastest.
Arguments:
- nodes: bfloat16 [131072, 9, 128], P(('slab', 'graph')), may hold values from -6 to 6
- boundary: int32 [128, 2, 640], P('slab'), may hold values from 0 to 1023
- sources: int32 [655360], P(('slab', 'graph')), may hold values from 0 to 2303
- targets: int32 [655360], P(('slab', 'graph')), may hold values from 0 to 1023
- block_counts: int32 [128, 2], replicated, may hold values from 10 to 20, as said below
- wigner: float32 [35, 655360], P(None, ('slab', 'graph')), may hold values from -3 to 3
- radial: bfloat16 [655360, 128], P(('slab', 'graph')), may hold values from -6 to 6
- w_zero: bfloat16 [384, 384], replicated, may hold values from -0.3125 to 0.3125
- w_one: bfloat16 [2, 256, 256], replicated, may hold values from -0.25 to 0.25
- w_two: bfloat16 [2, 128, 128], replicated, may hold values from -0.375 to 0.375
Outputs:
- updated: bfloat16 [131072, 9, 128], P(('slab', 'graph'))
Inputs may be any that keep to these rules, and one draw needn't show every extreme that they name: Slots of device (s, g) from block_counts[s, g] * 128 on are padding; every draw has some device with 20 live blocks.
All inputs are finite; a program needn't handle non-finite values.
Results may differ from a plain program's by a relative error of at most 0.0064.
Values may be sent and summed in bfloat16 or wider, within the bound.
A program may use at most 64 MiB of HBM per device.

v0:
```python
import jax
import jax.numpy as jnp
from jax import lax
from jax.sharding import PartitionSpec as P

EDGE_BLOCK = 128
GROUP_BLOCKS = 4


message_scale = 0.2
wigner_blocks = ((0, 0, 1), (1, 1, 3), (10, 4, 5))


def shifted(x, axis, by):
    size = lax.axis_size(axis)
    return lax.ppermute(x, axis, [(i, (i + by) % size) for i in range(size)])


def rotate(coeffs, wig_rows, inverse):
    out_list = []
    for offset, first_coef, block_size in wigner_blocks:
        for row_index in range(block_size):
            summed = None
            for col_index in range(block_size):
                if inverse:
                    entry_index = offset + col_index * block_size + row_index
                else:
                    entry_index = offset + row_index * block_size + col_index
                product_term = wig_rows[entry_index][:, None] * coeffs[:, first_coef + col_index, :]
                summed = product_term if summed is None else summed + product_term
            out_list.append(summed)
    return jnp.stack(out_list, axis=1)


def build_pair(pair_weights):
    real_part = pair_weights[0]
    imag_part = pair_weights[1]
    top_half = jnp.concatenate([real_part, imag_part], axis=1)
    low_half = jnp.concatenate([-imag_part, real_part], axis=1)
    return jnp.concatenate([top_half, low_half], axis=0)


def mix_orders(rotated, w_zero, pair_one, pair_two):
    chan = rotated.shape[2]
    zero_in = jnp.concatenate([rotated[:, 0], rotated[:, 2], rotated[:, 6]], axis=1)
    zero_out = jnp.dot(zero_in, w_zero, preferred_element_type=jnp.float32)
    one_in = jnp.concatenate([rotated[:, 3], rotated[:, 7], rotated[:, 1], rotated[:, 5]], axis=1)
    one_out = jnp.dot(one_in, pair_one, preferred_element_type=jnp.float32)
    two_in = jnp.concatenate([rotated[:, 8], rotated[:, 4]], axis=1)
    two_out = jnp.dot(two_in, pair_two, preferred_element_type=jnp.float32)
    pieces = [
        zero_out[:, :chan],
        one_out[:, 2 * chan : 3 * chan],
        zero_out[:, chan : 2 * chan],
        one_out[:, :chan],
        two_out[:, chan:],
        one_out[:, 3 * chan :],
        zero_out[:, 2 * chan :],
        one_out[:, chan : 2 * chan],
        two_out[:, :chan],
    ]
    return jnp.stack(pieces, axis=1).astype(jnp.bfloat16)


def front(src_rows, wig_rows, rad_rows):
    turned = rotate(src_rows.astype(jnp.float32), wig_rows, False)
    return (turned * rad_rows.astype(jnp.float32)[:, None, :]).astype(jnp.bfloat16)


def finish(mixed, wig_rows, live_mask):
    turned = rotate(mixed.astype(jnp.float32), wig_rows, True)
    return (turned * live_mask[:, None, None]).astype(jnp.bfloat16)


def scatter_rows(partial_value, messages, tgt_rows):
    slab_atoms = partial_value.shape[0]
    onehot = (tgt_rows[:, None] == jnp.arange(slab_atoms, dtype=jnp.int32)[None, :]).astype(
        jnp.bfloat16
    )
    flat = messages.reshape(messages.shape[0], -1)
    return partial_value + lax.dot_general(
        onehot, flat, (((0,), (0,)), ((), ())), preferred_element_type=jnp.float32
    )


def accumulate(partial_value, base, live_edges, make_mixed, targets, wigner):
    group_rows = GROUP_BLOCKS * EDGE_BLOCK
    positions = jnp.arange(group_rows, dtype=jnp.int32)

    def one_group(group_index, carried):
        offset = base + group_index * group_rows
        wig_rows = lax.dynamic_slice_in_dim(wigner, offset, group_rows, 1)
        tgt_rows = lax.dynamic_slice_in_dim(targets, offset, group_rows, 0)
        live_mask = (group_index * group_rows + positions < live_edges).astype(jnp.float32)
        messages = finish(make_mixed(offset, wig_rows), wig_rows, live_mask)
        return scatter_rows(carried, messages, tgt_rows)

    group_count = (live_edges + group_rows - 1) // group_rows
    return lax.fori_loop(0, group_count, one_group, partial_value)


def per_device(
    nodes, boundary, sources, targets, block_counts, wigner, radial, w_zero, w_one, w_two
):
    pair_one = build_pair(w_one)
    pair_two = build_pair(w_two)
    group_rows = GROUP_BLOCKS * EDGE_BLOCK
    slab_rows = lax.all_gather(nodes, "graph", axis=0, tiled=True)
    upper_rows = jnp.take(slab_rows, boundary[0, 1], axis=0)
    lower_rows = jnp.take(slab_rows, boundary[0, 0], axis=0)
    from_below = shifted(upper_rows, "slab", 1)
    from_above = shifted(lower_rows, "slab", -1)
    lookup = jnp.concatenate([slab_rows, from_below, from_above], axis=0)
    slab_index = lax.axis_index("slab")
    graph_index = lax.axis_index("graph")
    own_edges = block_counts[slab_index, graph_index] * EDGE_BLOCK

    def local_mixed(offset, wig_rows):
        src_index = lax.dynamic_slice_in_dim(sources, offset, group_rows, 0)
        rad_rows = lax.dynamic_slice_in_dim(radial, offset, group_rows, 0)
        turned = front(jnp.take(lookup, src_index, axis=0), wig_rows, rad_rows)
        return mix_orders(turned, w_zero, pair_one, pair_two)

    partial_value = jnp.zeros((slab_rows.shape[0], 9 * nodes.shape[2]), jnp.float32)
    partial_value = accumulate(partial_value, 0, own_edges, local_mixed, targets, wigner)
    summed = lax.psum_scatter(partial_value, "graph", scatter_dimension=0, tiled=True)
    return (summed * message_scale).astype(jnp.bfloat16).reshape(nodes.shape)


def solution(mesh):
    return jax.shard_map(
        per_device,
        mesh=mesh,
        in_specs=(
            P(("slab", "graph"), None, None),
            P("slab", None, None),
            P(("slab", "graph")),
            P(("slab", "graph")),
            P(),
            P(None, ("slab", "graph")),
            P(("slab", "graph"), None),
            P(),
            P(),
            P(),
        ),
        out_specs=P(("slab", "graph"), None, None),
        check_vma=False,
    )
```

profile of v0, /device:TPU:1, one launch (start us, length us, event | category | flops | bytes accessed | tf_op | source)
XLA Modules:
  0.0 311.7 jit_solution(17379629399174327335)
XLA Ops:
  8.1 21.8 %all-gather.2.cloned.1.call-done = bf16[1024,9,128]{2,0,1:T(8,128)(2,1)} async-done(((bf16[512,9,128]{2,0,1:T(8,128)(2,1)}), bf16[1024,9,128]{2,0,1:T(8,128)(2,1)}) %all-gather.2.cloned.1.call-update) | async-done | bytes 2359312 | tf_op jit(solution)/shard_map/all_gather | solution.py:108
  30.0 5.4 %copy.24 = bf16[1024,9,128]{2,1,0:T(8,128)(2,1)} copy(bf16[1024,9,128]{2,0,1:T(8,128)(2,1)} %all-gather.2.cloned.1.call-done) | data formatting | bytes 4718592 | tf_op jit(solution)/shard_map/all_gather | solution.py:108
  35.4 3.5 %gather_fusion.1 = bf16[640,9,128]{2,1,0:T(8,128)(2,1)S(1)} fusion(bf16[1024,9,128]{2,1,0:T(8,128)(2,1)} %copy.24, s32[1024]{0:T(1024)S(1)} %pad_clamp_fusion.2), kind=kCustom, calls=%fused_computation.clone | custom fusion | bytes 2951680 | tf_op jit(solution)/shard_map/jit(_take)/gather | solution.py:109
  38.9 2.3 broadcast_select_fusion.1
  41.2 1.6 copy.25
  43.8 3.5 %gather_fusion.2 = bf16[640,9,128]{2,1,0:T(8,128)(2,1)S(1)} fusion(bf16[1024,9,128]{2,1,0:T(8,128)(2,1)} %copy.24, s32[1024]{0:T(1024)S(1)} %pad_clamp_fusion.1), kind=kCustom, calls=%fused_computation.2.clone | custom fusion | bytes 2951680 | tf_op jit(solution)/shard_map/jit(_take)/gather | solution.py:110
  47.4 2.3 broadcast_select_fusion
  51.2 6.1 %collective-permute-start.1 = (bf16[640,9,128]{2,0,1:T(8,128)(2,1)}, bf16[640,9,128]{2,0,1:T(8,128)(2,1)}, u32[]{:S(2)}, u32[]{:S(2)}) collective-permute-start(bf16[640,9,128]{2,0,1:T(8,128)(2,1)} %copy.27), channel_id=1, source_target_pairs={{0,254},{2,0},{4,2},{6,4},{8,6},{10,8},{12,10},{14,12},{16,14},{18... | collective-permute-start | bytes 4423688 | tf_op jit(solution)/shard_map/ppermute | solution.py:16
  60.2 22.4 %collective-permute-done = bf16[640,9,128]{2,0,1:T(8,128)(2,1)} collective-permute-done((bf16[640,9,128]{2,0,1:T(8,128)(2,1)}, bf16[640,9,128]{2,0,1:T(8,128)(2,1)}, u32[]{:S(2)}, u32[]{:S(2)}) %collective-permute-start) | collective-permute-done | bytes 1474592 | tf_op jit(solution)/shard_map/ppermute | solution.py:16
  82.6 6.4 %collective-permute-done.1 = bf16[640,9,128]{2,0,1:T(8,128)(2,1)} collective-permute-done((bf16[640,9,128]{2,0,1:T(8,128)(2,1)}, bf16[640,9,128]{2,0,1:T(8,128)(2,1)}, u32[]{:S(2)}, u32[]{:S(2)}) %collective-permute-start.1) | collective-permute-done | bytes 1474592 | tf_op jit(solution)/shard_map/ppermute | solution.py:16
  89.0 2.7 pad_maximum_fusion
  91.7 26.3 %copy.28 = bf16[2304,9,128]{2,1,0:T(8,128)(2,1)} copy(bf16[2304,9,128]{2,0,1:T(8,128)(2,1)S(1)} %pad_maximum_fusion) | data formatting | bytes 10616832
  118.0 2.5 broadcast_in_dim.28
  120.5 157.0 %while.11 = (s32[]{:T(128)}, f32[1024,1152]{1,0:T(8,128)}, s32[]{:T(128)}, s32[2560]{0:T(1024)}, f32[35,2560]{1,0:T(8,128)}, /*index=5*/s32[2560]{0:T(1024)}, bf...) while((s32[]{:T(128)}, f32[1024,1152]{1,0:T(8,128)}, ...), condition=%wide.region_1.3_spmd.clone, body=%wide.region_0.0_spmd.clone.sunk | while | flops 1713313280 | bytes 65880160 | solution.py:99
  121.3 4.9 %gather_fusion = bf16[512,9,128]{2,1,0:T(8,128)(2,1)S(1)} fusion(bf16[2304,9,128]{2,1,0:T(8,128)(2,1)} %get-tuple-element.505, s32[1024]{0:T(1024)S(1)} %pad_clamp_fusion.4), kind=kCustom, calls=%fused_computation.1.clone.clone.1 | custom fusion | bytes 2361344 | tf_op jit(solution)/shard_map/while/body/jit(_take)/gather | solution.py:121
  139.0 2.0 multiply_convert_fusion.3
  145.6 6.3 %convolution_add_fusion.2 = f32[1024,1152]{1,0:T(8,128)} fusion(f32[1024,1152]{1,0:T(8,128)} %get-tuple-element.450, bf16[512,1152]{0,1:T(8,128)(2,1)S(1)} %fusion.88, s32[512]{0:T(512)S(1)} %dynamic_slice.26), kind=kOutput, calls=%fused_computation.4.clone.1 | convolution fusion | flops 1210187776 | bytes 10618880 | tf_op jit(solution)/shard_map/while/body/dot_general | solution.py:81
  152.7 4.9 %gather_fusion = bf16[512,9,128]{2,1,0:T(8,128)(2,1)S(1)} fusion(bf16[2304,9,128]{2,1,0:T(8,128)(2,1)} %get-tuple-element.505, s32[1024]{0:T(1024)S(1)} %pad_clamp_fusion.4), kind=kCustom, calls=%fused_computation.1.clone.clone.1 | custom fusion | bytes 2361344 | tf_op jit(solution)/shard_map/while/body/jit(_take)/gather | solution.py:121
  170.4 2.0 multiply_convert_fusion.3
  177.1 6.3 %convolution_add_fusion.2 = f32[1024,1152]{1,0:T(8,128)} fusion(f32[1024,1152]{1,0:T(8,128)} %get-tuple-element.450, bf16[512,1152]{0,1:T(8,128)(2,1)S(1)} %fusion.88, s32[512]{0:T(512)S(1)} %dynamic_slice.26), kind=kOutput, calls=%fused_computation.4.clone.1 | convolution fusion | flops 1210187776 | bytes 10618880 | tf_op jit(solution)/shard_map/while/body/dot_general | solution.py:81
  184.1 4.9 %gather_fusion = bf16[512,9,128]{2,1,0:T(8,128)(2,1)S(1)} fusion(bf16[2304,9,128]{2,1,0:T(8,128)(2,1)} %get-tuple-element.505, s32[1024]{0:T(1024)S(1)} %pad_clamp_fusion.4), kind=kCustom, calls=%fused_computation.1.clone.clone.1 | custom fusion | bytes 2361344 | tf_op jit(solution)/shard_map/while/body/jit(_take)/gather | solution.py:121
  201.8 2.0 multiply_convert_fusion.3
  208.5 6.3 %convolution_add_fusion.2 = f32[1024,1152]{1,0:T(8,128)} fusion(f32[1024,1152]{1,0:T(8,128)} %get-tuple-element.450, bf16[512,1152]{0,1:T(8,128)(2,1)S(1)} %fusion.88, s32[512]{0:T(512)S(1)} %dynamic_slice.26), kind=kOutput, calls=%fused_computation.4.clone.1 | convolution fusion | flops 1210187776 | bytes 10618880 | tf_op jit(solution)/shard_map/while/body/dot_general | solution.py:81
  215.6 4.9 %gather_fusion = bf16[512,9,128]{2,1,0:T(8,128)(2,1)S(1)} fusion(bf16[2304,9,128]{2,1,0:T(8,128)(2,1)} %get-tuple-element.505, s32[1024]{0:T(1024)S(1)} %pad_clamp_fusion.4), kind=kCustom, calls=%fused_computation.1.clone.clone.1 | custom fusion | bytes 2361344 | tf_op jit(solution)/shard_map/while/body/jit(_take)/gather | solution.py:121
  233.3 2.0 multiply_convert_fusion.3
  239.9 6.3 %convolution_add_fusion.2 = f32[1024,1152]{1,0:T(8,128)} fusion(f32[1024,1152]{1,0:T(8,128)} %get-tuple-element.450, bf16[512,1152]{0,1:T(8,128)(2,1)S(1)} %fusion.88, s32[512]{0:T(512)S(1)} %dynamic_slice.26), kind=kOutput, calls=%fused_computation.4.clone.1 | convolution fusion | flops 1210187776 | bytes 10618880 | tf_op jit(solution)/shard_map/while/body/dot_general | solution.py:81
  247.0 4.9 %gather_fusion = bf16[512,9,128]{2,1,0:T(8,128)(2,1)S(1)} fusion(bf16[2304,9,128]{2,1,0:T(8,128)(2,1)} %get-tuple-element.505, s32[1024]{0:T(1024)S(1)} %pad_clamp_fusion.4), kind=kCustom, calls=%fused_computation.1.clone.clone.1 | custom fusion | bytes 2361344 | tf_op jit(solution)/shard_map/while/body/jit(_take)/gather | solution.py:121
  264.5 2.0 multiply_convert_fusion.3
  271.2 6.3 %convolution_add_fusion.2 = f32[1024,1152]{1,0:T(8,128)} fusion(f32[1024,1152]{1,0:T(8,128)} %get-tuple-element.450, bf16[512,1152]{0,1:T(8,128)(2,1)S(1)} %fusion.88, s32[512]{0:T(512)S(1)} %dynamic_slice.26), kind=kOutput, calls=%fused_computation.4.clone.1 | convolution fusion | flops 1210187776 | bytes 10618880 | tf_op jit(solution)/shard_map/while/body/dot_general | solution.py:81
  277.5 6.1 %copy.30 = f32[1024,1152]{0,1:T(8,128)} copy(f32[1024,1152]{1,0:T(8,128)} %get-tuple-element.74) | data formatting | bytes 9437184 | tf_op jit(solution)/shard_map/while | solution.py:99
  283.6 17.9 %reduce-scatter.2.cloned.1.call-done = f32[512,1152]{0,1:T(8,128)} async-done(((f32[1024,1152]{0,1:T(8,128)}), f32[512,1152]{0,1:T(8,128)}) %reduce-scatter.2.cloned.1.call-update) | async-done | bytes 2359312 | tf_op jit(solution)/shard_map/reduce_scatter | solution.py:126
  301.5 2.0 multiply_convert_fusion.1
  (272 shorter events, 97.1 us)
Async XLA Ops:
  6.5 23.4 %all-gather.2.cloned.1.call-start = ((), (), s32[]{:S(2)}) async-start(), calls=%async_computation.1 | async-start | bytes 3538944 | tf_op jit(solution)/shard_map/all_gather | solution.py:108
  7.3 294.2 %reduce-scatter.2.cloned.1.call-start = ((), (), s32[]{:S(2)}) async-start(), calls=%async_computation.2 | async-start | bytes 7077888 | tf_op jit(solution)/shard_map/reduce_scatter | solution.py:126
  42.9 39.7 %collective-permute-start = (bf16[640,9,128]{2,0,1:T(8,128)(2,1)}, bf16[640,9,128]{2,0,1:T(8,128)(2,1)}, u32[]{:S(2)}, u32[]{:S(2)}) collective-permute-start(bf16[640,9,128]{2,0,1:T(8,128)(2,1)} %copy.25), channel_id=1, source_target_pairs={{0,2},{2,4},{4,6},{6,8},{8,10},{10,12},{12,14},{14,16},{16,18},{18... | collective-permute-start | bytes 4423688 | tf_op jit(solution)/shard_map/ppermute | solution.py:16
  49.7 7.7 %copy-start.5 = (s32[128,2]{0,1:T(2,128)S(1)}, s32[128,2]{0,1:T(2,128)}, u32[]{:S(2)}) copy-start(s32[128,2]{0,1:T(2,128)} %param.18) | copy-start | bytes 3076
  49.7 8.9 %copy-start.3 = (bf16[2,128,128]{2,1,0:T(8,128)(2,1)S(1)}, bf16[2,128,128]{2,1,0:T(8,128)(2,1)}, u32[]{:S(2)}) copy-start(bf16[2,128,128]{2,1,0:T(8,128)(2,1)} %param.23) | copy-start | bytes 196612
  49.7 9.6 %copy-start.1 = (bf16[2,256,256]{2,1,0:T(8,128)(2,1)S(1)}, bf16[2,256,256]{2,1,0:T(8,128)(2,1)}, u32[]{:S(2)}) copy-start(bf16[2,256,256]{2,1,0:T(8,128)(2,1)} %param.22) | copy-start | bytes 786436
  49.7 39.3 %copy-start = (bf16[1024,9,128]{2,0,1:T(8,128)(2,1)S(1)}, bf16[1024,9,128]{2,0,1:T(8,128)(2,1)}, u32[]{:S(2)}) copy-start(bf16[1024,9,128]{2,0,1:T(8,128)(2,1)} %all-gather.2.cloned.1.call-done) | copy-start | bytes 7077892
  51.2 37.8 %collective-permute-start.1 = (bf16[640,9,128]{2,0,1:T(8,128)(2,1)}, bf16[640,9,128]{2,0,1:T(8,128)(2,1)}, u32[]{:S(2)}, u32[]{:S(2)}) collective-permute-start(bf16[640,9,128]{2,0,1:T(8,128)(2,1)} %copy.27), channel_id=1, source_target_pairs={{0,254},{2,0},{4,2},{6,4},{8,6},{10,8},{12,10},{14,12},{16,14},{18... | collective-permute-start | bytes 4423688 | tf_op jit(solution)/shard_map/ppermute | solution.py:16
  139.0 2.2 copy-start.4
  141.0 1.0 copy-start.2
  141.2 1.4 copy-start.6
  170.4 2.2 copy-start.4
  172.5 1.0 copy-start.2
  172.6 1.4 copy-start.6
  201.8 2.2 copy-start.4
  203.9 1.0 copy-start.2
  204.0 1.4 copy-start.6
  233.3 2.2 copy-start.4
  235.3 1.0 copy-start.2
  235.5 1.4 copy-start.6
  264.5 2.2 copy-start.4
  266.6 1.0 copy-start.2
  266.7 1.4 copy-start.6
Sparse Core Ops, SparseCore 0:
  9.1 20.7 all-gather.1
  283.7 17.6 reduce-scatter.1
where the time goes:
time: 315 us; the launch traced here: 312 us
  local copies, waits for them, and re-layouts  112 us (36%)
  other arithmetic  70.7 us (22%)
  waiting for transfers between devices  69.2 us (22%)
  matrix products  37.4 us (12%)
  between operations  14.2 us (5%)
  starting transfers between devices  7.12 us (2%)
    while x80, other arithmetic  36.7 us
    gather x10, local copies, waits for them, and re-layouts, local_mixed(): turned = front(jnp.take(lookup, src_index, axis=0), wig_rows, rad_rows)  31.6 us
    dot_general x5, matrix products, scatter_rows(): lax.dot_general(onehot, flat, (((0,), (0,)), ((), ())), preferred_element...  31.6 us
    ppermute x2, waiting for transfers between devices, shifted(): return lax.ppermute(x, axis, [(i, (i + by) % size) for i in range(size)])  28.8 us
    unnamed x9, local copies, waits for them, and re-layouts  26.3 us
    all_gather x1, waiting for transfers between devices, per_device(): slab_rows = lax.all_gather(nodes, 'graph', axis=0, tiled=True)  21.8 us
    reduce_scatter x1, waiting for transfers between devices, per_device(): lax.psum_scatter(partial_value, 'graph', scatter_dimension=0, tiled=True)  17.9 us
    slice x10, local copies, waits for them, and re-layouts, rotate(): wig_rows[entry_index][:, None] * coeffs[:, first_coef + col_index, :]  13.5 us
  transfers between devices with their start and end apart: 4, of which 4 were waited for; matrix products, arithmetic and copies ran while one was open for 3% of the time, Pallas kernels for 0%

commit v1 on v0

v1 whole, which is shorter than its diff:
```python
import jax
import jax.numpy as jnp
from jax import lax
from jax.experimental import pallas as pl
from jax.experimental.pallas import tpu as pltpu
from jax.sharding import PartitionSpec as P

EDGE_BLOCK = 128
ROWS = 9
BLOCKS = ((0, 0, 1), (1, 1, 3), (10, 4, 5))
PLACE = {0: 0, 2: 1, 6: 2, 3: 3, 7: 4, 1: 5, 5: 6, 8: 7, 4: 8}
MESH = pl.DeviceIdType.MESH
message_scale = 0.2
CHUNK = 64


def layer_kernel(
    boundary, src, counts, nodes, tgt, wig, rad, w_zero, w_one, w_two, out,
    table, other, send_up, send_down, from_below, from_above, stage, wscr, spread,
    turned, mixed, msgs, onehot, pair_one, pair_two, sums, arrived,
    n_send, n_recv, up_send, up_recv, down_send, down_recv,
    fb_send, fb_recv, fa_send, fa_recv, s_send, s_recv,
):
    n_slab = lax.axis_size("slab")
    s = lax.axis_index("slab")
    g = lax.axis_index("graph")
    up = lax.rem(s + 1, n_slab)
    down = lax.rem(s + n_slab - 1, n_slab)
    mate = 1 - g
    half = nodes.shape[1]
    slab_atoms = 2 * half
    face = boundary.shape[1]
    mine = face // 2
    edges = src.shape[0]
    chan = nodes.shape[2]
    n_chunk = mine // CHUNK
    crows = CHUNK * ROWS

    barrier = pltpu.get_barrier_semaphore()
    for where in ((s, mate), (up, g), (down, g)):
        pl.semaphore_signal(barrier, inc=1, device_id=where, device_id_type=MESH)
    pl.semaphore_wait(barrier, 3)

    swap = pltpu.make_async_remote_copy(
        src_ref=nodes, dst_ref=other, send_sem=n_send, recv_sem=n_recv,
        device_id=(s, mate), device_id_type=MESH)
    swap.start()

    def fill(planes, first):
        def step(i, _):
            at = pl.multiple_of(i * 16, 16)
            for c in range(ROWS):
                table[pl.ds((first + at) * ROWS + c, 16, stride=ROWS), :] = (
                    planes[c, pl.ds(at, 16), :].astype(jnp.float32))
            return 0
        lax.fori_loop(0, half // 16, step, 0, unroll=2)

    fill(nodes, g * half)

    width = w_one.shape[1]
    pair_one[0:width, 0:width] = w_one[0]
    pair_one[0:width, width:] = w_one[1]
    pair_one[width:, 0:width] = -w_one[1]
    pair_one[width:, width:] = w_one[0]
    pair_two[0:chan, 0:chan] = w_two[0]
    pair_two[0:chan, chan:] = w_two[1]
    pair_two[chan:, 0:chan] = -w_two[1]
    pair_two[chan:, chan:] = w_two[0]
    wscr[...] = jnp.zeros_like(wscr)

    swap.wait()
    fill(other, mate * half)

    def take_rows(row_of, first, count):
        def step(i, _):
            r = row_of(first + i) * ROWS
            stage[pl.ds(i * ROWS, 8), :] = table[pl.ds(r, 8), :]
            stage[pl.ds(i * ROWS + 8, 1), :] = table[pl.ds(r + 8, 1), :]
            return 0
        lax.fori_loop(0, count, step, 0, unroll=16)

    def face_copy(k, buf, dst, ss, rs, to):
        return pltpu.make_async_remote_copy(
            src_ref=buf.at[pl.ds(pl.multiple_of(k * crows, crows), crows), :],
            dst_ref=dst.at[pl.ds(pl.multiple_of((g * n_chunk + k) * crows, crows), crows), :],
            send_sem=ss.at[k], recv_sem=rs.at[k], device_id=(to, g), device_id_type=MESH)

    def send_face(k, _):
        for side, buf, dst, ss, rs, to in (
            (1, send_up, from_below, up_send, up_recv, up),
            (0, send_down, from_above, down_send, down_recv, down)):
            take_rows(lambda i: boundary[side, i], g * mine + k * CHUNK, CHUNK)
            buf[pl.ds(pl.multiple_of(k * crows, crows), crows), :] = (
                stage[0:crows, :].astype(jnp.bfloat16))
            face_copy(k, buf, dst, ss, rs, to).start()
        return 0

    lax.fori_loop(0, n_chunk, send_face, 0)

    live = counts[s, g] * EDGE_BLOCK
    slot = lax.broadcasted_iota(jnp.int32, (1, edges), 1)
    goal = jnp.where(slot < live, tgt[...], -1)

    def mark(i, _):
        at = pl.multiple_of(i * 16, 16)
        first = jnp.where(at < half, mate * half + at, g * half + at - half)
        atom = first + lax.broadcasted_iota(jnp.int32, (16, edges), 0)
        onehot[pl.ds(at, 16), :] = jnp.where(atom == goal, 1.0, 0.0).astype(jnp.bfloat16)
        return 0

    lax.fori_loop(0, slab_atoms // 16, mark, 0)

    def forward(k, buf, ss, rs):
        part = buf.at[pl.ds(pl.multiple_of((g * n_chunk + k) * crows, crows), crows), :]
        return pltpu.make_async_remote_copy(
            src_ref=part, dst_ref=part, send_sem=ss.at[k], recv_sem=rs.at[k],
            device_id=(s, mate), device_id_type=MESH)

    def widen(buf, at, base):
        table[pl.ds(base + at, crows), :] = buf[pl.ds(pl.multiple_of(at, crows), crows), :].astype(jnp.float32)

    sides = (
        (send_up, from_below, up_send, up_recv, up, fb_send, fb_recv, slab_atoms * ROWS),
        (send_down, from_above, down_send, down_recv, down, fa_send, fa_recv, (slab_atoms + face) * ROWS),
    )

    def land(k, _):
        for buf, dst, ss, rs, to, fs, fr, base in sides:
            face_copy(k, buf, dst, ss, rs, to).wait()
            forward(k, dst, fs, fr).start()
            widen(dst, (g * n_chunk + k) * crows, base)
        return 0

    lax.fori_loop(0, n_chunk, land, 0)

    def finish_land(k, _):
        for buf, dst, ss, rs, to, fs, fr, base in sides:
            forward(k, dst, fs, fr).wait()
            widen(dst, (mate * n_chunk + k) * crows, base)
        return 0

    lax.fori_loop(0, n_chunk, finish_land, 0)

    G = 16

    def block(b, _):
        base = pl.multiple_of(b * EDGE_BLOCK, EDGE_BLOCK)
        take_rows(lambda i: src[i], base, EDGE_BLOCK)
        wscr[0:35, :] = wig[:, pl.ds(base, EDGE_BLOCK)]
        wt = wscr[...].T
        for k in range(35):
            spread[k] = jnp.broadcast_to(wt[:, k:k + 1], (EDGE_BLOCK, chan))
        for q in range(EDGE_BLOCK // G):
            rows = slice(q * G, (q + 1) * G)
            rr = rad[pl.ds(base + q * G, G), :].astype(jnp.float32)
            xs = [stage[pl.ds(q * G * ROWS + c, G, stride=ROWS), :] for c in range(ROWS)]
            for off, first, n in BLOCKS:
                for i in range(n):
                    acc = None
                    for j in range(n):
                        term = spread[off + i * n + j, rows, :] * xs[first + j]
                        acc = term if acc is None else acc + term
                    at = PLACE[first + i] * chan
                    turned[rows, at:at + chan] = (acc * rr).astype(jnp.bfloat16)
        mixed[:, 0:3 * chan] = jnp.dot(turned[:, 0:3 * chan], w_zero[...], preferred_element_type=jnp.float32)
        mixed[:, 3 * chan:7 * chan] = jnp.dot(
            turned[:, 3 * chan:7 * chan], pair_one[...], preferred_element_type=jnp.float32)
        mixed[:, 7 * chan:] = jnp.dot(turned[:, 7 * chan:], pair_two[...], preferred_element_type=jnp.float32)
        for q in range(EDGE_BLOCK // G):
            rows = slice(q * G, (q + 1) * G)
            xs = [mixed[rows, PLACE[c] * chan:(PLACE[c] + 1) * chan] for c in range(ROWS)]
            for off, first, n in BLOCKS:
                for i in range(n):
                    acc = None
                    for j in range(n):
                        term = spread[off + j * n + i, rows, :] * xs[first + j]
                        acc = term if acc is None else acc + term
                    c = first + i
                    msgs[c // 2, pl.ds(base + q * G, G), (c % 2) * chan:(c % 2 + 1) * chan] = (
                        acc.astype(jnp.bfloat16))
        return 0

    lax.fori_loop(0, edges // EDGE_BLOCK, block, 0)

    def hand_over(p, w):
        return pltpu.make_async_remote_copy(
            src_ref=sums.at[p, :, pl.ds(0, w)], dst_ref=arrived.at[p, :, pl.ds(0, w)],
            send_sem=s_send.at[p], recv_sem=s_recv.at[p], device_id=(s, mate), device_id_type=MESH)

    widths = [2 * chan] * 4 + [chan]
    for p, w in enumerate(widths):
        sums[p, :, 0:w] = jnp.dot(onehot[0:half, :], msgs[p, :, 0:w], preferred_element_type=jnp.float32)
        hand_over(p, w).start()
    for p, w in enumerate(widths):
        own = jnp.dot(onehot[half:, :], msgs[p, :, 0:w], preferred_element_type=jnp.float32)
        hand_over(p, w).wait()
        total = ((own + arrived[p, :, 0:w]) * message_scale).astype(jnp.bfloat16)
        out[2 * p] = total[:, 0:chan]
        if w > chan:
            out[2 * p + 1] = total[:, chan:]


def per_device(nodes, boundary, sources, targets, block_counts, wigner, radial, w_zero, w_one, w_two):
    half, rows, chan = nodes.shape
    edges = sources.shape[0]
    face = boundary.shape[2]
    n_chunk = face // 2 // CHUNK
    atoms = 2 * half
    vm = pl.BlockSpec(memory_space=pltpu.VMEM)
    sm = pl.BlockSpec(memory_space=pltpu.SMEM)
    dma = pltpu.SemaphoreType.DMA
    out = pl.pallas_call(
        layer_kernel,
        out_shape=jax.ShapeDtypeStruct((rows, half, chan), jnp.bfloat16),
        in_specs=[sm, sm, sm] + [vm] * 7,
        out_specs=vm,
        scratch_shapes=[
            pltpu.VMEM(((atoms + 2 * face) * rows, chan), jnp.float32),
            pltpu.VMEM((rows, half, chan), jnp.bfloat16),
            pltpu.VMEM((face // 2 * rows, chan), jnp.bfloat16),
            pltpu.VMEM((face // 2 * rows, chan), jnp.bfloat16),
            pltpu.VMEM((face * rows, chan), jnp.bfloat16),
            pltpu.VMEM((face * rows, chan), jnp.bfloat16),
            pltpu.VMEM((EDGE_BLOCK * rows, chan), jnp.float32),
            pltpu.VMEM((128, EDGE_BLOCK), jnp.float32),
            pltpu.VMEM((35, EDGE_BLOCK, chan), jnp.float32),
            pltpu.VMEM((EDGE_BLOCK, rows * chan), jnp.bfloat16),
            pltpu.VMEM((EDGE_BLOCK, rows * chan), jnp.float32),
            pltpu.VMEM((5, edges, 2 * chan), jnp.bfloat16),
            pltpu.VMEM((atoms, edges), jnp.bfloat16),
            pltpu.VMEM((4 * chan, 4 * chan), jnp.bfloat16),
            pltpu.VMEM((2 * chan, 2 * chan), jnp.bfloat16),
            pltpu.VMEM((5, half, 2 * chan), jnp.float32),
            pltpu.VMEM((5, half, 2 * chan), jnp.float32),
            dma, dma,
            dma((n_chunk,)), dma((n_chunk,)), dma((n_chunk,)), dma((n_chunk,)),
            dma((n_chunk,)), dma((n_chunk,)), dma((n_chunk,)), dma((n_chunk,)),
            dma((5,)), dma((5,)),
        ],
        compiler_params=pltpu.CompilerParams(
            collective_id=0, has_side_effects=True, vmem_limit_bytes=62 * 1024 * 1024),
        name="layer",
    )(boundary[0], sources, block_counts, jnp.transpose(nodes, (1, 0, 2)), targets[None, :],
      wigner, radial, w_zero, w_one, w_two)
    return jnp.transpose(out, (1, 0, 2))


def solution(mesh):
    return jax.shard_map(
        per_device,
        mesh=mesh,
        in_specs=(
            P(("slab", "graph"), None, None),
            P("slab", None, None),
            P(("slab", "graph")),
            P(("slab", "graph")),
            P(),
            P(None, ("slab", "graph")),
            P(("slab", "graph"), None),
            P(),
            P(),
            P(),
        ),
        out_specs=P(("slab", "graph"), None, None),
        check_vma=False,
    )
```

time: 315 us -> 85.2 us (0.27)
  local copies, waits for them, and re-layouts: 112 us -> 5.08 us
  Pallas kernels: 0 us -> 79.9 us
  other arithmetic: 70.7 us -> 0 us
  waiting for transfers between devices: 69.2 us -> 0 us
  matrix products: 37.4 us -> 0 us
  between operations: 14.2 us -> 0.01 us
  starting transfers between devices: 7.12 us -> 0 us
    pallas_call x0 -> x1, Pallas kernels: none -> 79.9 us  [per_device(): pl.pallas_call(layer_kernel, out_shape=jax.ShapeDtypeStruct((rows, half,...]
    gather x12 -> x0, local copies, waits for them, and re-layouts: 38.7 us -> none  [the longest x10 31.6 us: local_mixed(): turned = front(jnp.take(lookup, src_index, axis=0), wig_rows, rad_rows)]
    dot_general x20 -> x0, matrix products: 37.4 us -> none  [the longest x5 31.6 us: scatter_rows(): lax.dot_general(onehot, flat, (((0,), (0,)), ((), ())), preferred_element...]
    while x80 -> x0, other arithmetic: 36.7 us -> none
    ppermute x2 -> x0, waiting for transfers between devices: 28.8 us -> none  [shifted(): return lax.ppermute(x, axis, [(i, (i + by) % size) for i in range(size)])]
    unnamed x9 -> x2, local copies, waits for them, and re-layouts: 26.3 us -> 3.77 us
    all_gather x1 -> x0, waiting for transfers between devices: 21.8 us -> none  [per_device(): slab_rows = lax.all_gather(nodes, 'graph', axis=0, tiled=True)]
    reduce_scatter x1 -> x0, waiting for transfers between devices: 17.9 us -> none  [per_device(): lax.psum_scatter(partial_value, 'graph', scatter_dimension=0, tiled=True)]
  transfers between devices with their start and end apart: 4 -> 0, of which waited for: 4 -> 0; matrix products, arithmetic and copies ran while one was open for 3% -> 0% of each run, Pallas kernels for 0% -> 0%
where the time goes in v1:
time: 85.2 us; the launch traced here: 85 us
  Pallas kernels  79.9 us (94%)
  local copies, waits for them, and re-layouts  5.08 us (6%)
    pallas_call x1, Pallas kernels, per_device(): pl.pallas_call(layer_kernel, out_shape=jax.ShapeDtypeStruct((rows, half,...  79.9 us
    unnamed x2, local copies, waits for them, and re-layouts  3.77 us

profile of v1, /device:TPU:1, one launch (start us, length us, event | category | flops | bytes accessed | tf_op | source)
XLA Modules:
  0.0 85.0 jit_solution(15901080321817225201)
XLA Ops:
  0.0 1.3 %broadcast_in_dim.3.tgt = s32[1,2560]{1,0:T(1,128)} reshape(s32[2560]{0:T(1024)} %param.13) | data formatting | bytes 20480 | tf_op jit(solution)/shard_map/broadcast_in_dim | solution.py:243
  1.3 1.4 %copy.11.counts = s32[128,2]{1,0:T(8,128)} copy(s32[128,2]{0,1:T(2,128)} %param.14) | data formatting | bytes 2048 | tf_op args[4]
  2.7 79.9 %layer.1 = bf16[9,512,128]{2,1,0:T(8,128)(2,1)} custom-call(s32[2,640]{1,0:T(2,128)} %bitcast.5, s32[2560]{0:T(1024)} %src.1, s32[128,2]{1,0:T(8,128)} %copy.11.counts, bf16[9,512,128]{2,1,0:T(8,128)(2,1)} %bitcast.4, s32[1,2560]{1,0:T(1,128)} %broadcast_in_dim.3.tgt, f32[35,2560]{1,0:T(8,128)} %wig.1, bf16[2560,128]{1,0:T(8,128)(2,1)} %rad.1, ...), custom_call_target="tpu_custom_call" | custom-call | tf_op jit(solution)/shard_map/layer/pallas_call | solution.py:212
  82.6 2.4 %copy.13 = bf16[512,9,128]{2,0,1:T(8,128)(2,1)} copy(bf16[512,9,128]{2,0,1:T(8,128)(2,1)} %bitcast.3) | data formatting | bytes 2359296

commit v2 on v1

--- a/solution.py
+++ b/solution.py
@@ -1,3 +1,5 @@
+import functools
+
 import jax
 import jax.numpy as jnp
 from jax import lax
@@ -14,10 +16,16 @@
 CHUNK = 64
 
 
+def weave(*lists):
+    items = [((i + 0.5) / len(steps), k, i, step) for k, steps in enumerate(lists) for i, step in enumerate(steps)]
+    for item in sorted(items, key=lambda t: t[:3]):
+        item[3]()
+
+
 def layer_kernel(
     boundary, src, counts, nodes, tgt, wig, rad, w_zero, w_one, w_two, out,
-    table, other, send_up, send_down, from_below, from_above, stage, wscr, spread,
-    turned, mixed, msgs, onehot, pair_one, pair_two, sums, arrived,
+    table, other, send_up, send_down, from_below, from_above, stage, across, gain,
+    turned, mixed, msgs, onehot, wide_zero, wide_one, wide_two, sums, arrived,
     n_send, n_recv, up_send, up_recv, down_send, down_recv,
     fb_send, fb_recv, fa_send, fa_recv, s_send, s_recv,
 ):
@@ -58,26 +66,25 @@
     fill(nodes, g * half)
 
     width = w_one.shape[1]
-    pair_one[0:width, 0:width] = w_one[0]
-    pair_one[0:width, width:] = w_one[1]
-    pair_one[width:, 0:width] = -w_one[1]
-    pair_one[width:, width:] = w_one[0]
-    pair_two[0:chan, 0:chan] = w_two[0]
-    pair_two[0:chan, chan:] = w_two[1]
-    pair_two[chan:, 0:chan] = -w_two[1]
-    pair_two[chan:, chan:] = w_two[0]
-    wscr[...] = jnp.zeros_like(wscr)
+    wide_zero[...] = w_zero[...].T
+    real, imag = w_one[0].T, w_one[1].T
+    wide_one[0:width, 0:width] = real
+    wide_one[0:width, width:] = -imag
+    wide_one[width:, 0:width] = imag
+    wide_one[width:, width:] = real
+    real, imag = w_two[0].T, w_two[1].T
+    wide_two[0:chan, 0:chan] = real
+    wide_two[0:chan, chan:] = -imag
+    wide_two[chan:, 0:chan] = imag
+    wide_two[chan:, chan:] = real
 
     swap.wait()
     fill(other, mate * half)
 
-    def take_rows(row_of, first, count):
-        def step(i, _):
-            r = row_of(first + i) * ROWS
-            stage[pl.ds(i * ROWS, 8), :] = table[pl.ds(r, 8), :]
-            stage[pl.ds(i * ROWS + 8, 1), :] = table[pl.ds(r + 8, 1), :]
-            return 0
-        lax.fori_loop(0, count, step, 0, unroll=16)
+    def take_row(row, h, i):
+        r = row * ROWS
+        stage[h, pl.ds(i * ROWS, 8), :] = table[pl.ds(r, 8), :]
+        stage[h, pl.ds(i * ROWS + 8, 1), :] = table[pl.ds(r + 8, 1), :]
 
     def face_copy(k, buf, dst, ss, rs, to):
         return pltpu.make_async_remote_copy(
@@ -89,17 +96,20 @@
         for side, buf, dst, ss, rs, to in (
             (1, send_up, from_below, up_send, up_recv, up),
             (0, send_down, from_above, down_send, down_recv, down)):
-            take_rows(lambda i: boundary[side, i], g * mine + k * CHUNK, CHUNK)
+            def take(i, _):
+                take_row(boundary[side, g * mine + k * CHUNK + i], side, i)
+                return 0
+            lax.fori_loop(0, CHUNK, take, 0, unroll=16)
             buf[pl.ds(pl.multiple_of(k * crows, crows), crows), :] = (
-                stage[0:crows, :].astype(jnp.bfloat16))
+                stage[side, 0:crows, :].astype(jnp.bfloat16))
             face_copy(k, buf, dst, ss, rs, to).start()
         return 0
 
     lax.fori_loop(0, n_chunk, send_face, 0)
 
-    live = counts[s, g] * EDGE_BLOCK
+    live = counts[g, s] * EDGE_BLOCK
     slot = lax.broadcasted_iota(jnp.int32, (1, edges), 1)
-    goal = jnp.where(slot < live, tgt[...], -1)
+    goal = jnp.where(slot < live, tgt[...].reshape(1, edges), -1)
 
     def mark(i, _):
         at = pl.multiple_of(i * 16, 16)
@@ -142,57 +152,102 @@
     lax.fori_loop(0, n_chunk, finish_land, 0)
 
     G = 16
+    lanes = 128
+    width = 2 * lanes
+    n_block = edges // width
+
+    def gather(base, h):
+        def one(i):
+            return lambda: take_row(src[base + h * lanes + i], h, i)
+        return [one(i) for i in range(lanes)]
+
+    def turn(base, h):
+        def one(c):
+            def go():
+                across[h, c] = stage[h, pl.ds(c, lanes, stride=ROWS), :].T
+            return go
+
+        def radial():
+            gain[h] = rad[pl.ds(base + h * lanes, lanes), :].astype(jnp.float32).T
+        return [one(c) for c in range(ROWS)] + [radial]
+
+    def wide(k, at):
+        return jnp.broadcast_to(wig[k:k + 1, pl.ds(at, lanes)], (8, lanes))
+
+    def rotate(base, h, inverse):
+        at = base + h * lanes
+        cols = slice(h * lanes, (h + 1) * lanes)
+        steps = []
+        for off, first, n in BLOCKS:
+            held = {}
+
+            def go(q, off, first, n, held):
+                if q == 0:
+                    for k in range(n * n):
+                        held[k] = wide(off + k, at)
+                tops = (q * G, q * G + 8)
+                if inverse:
+                    xs = [[mixed[PLACE[first + j] * chan + t:PLACE[first + j] * chan + t + 8, cols] for t in tops]
+                          for j in range(n)]
+                else:
+                    xs = [[across[h, first + j, t:t + 8, :] for t in tops] for j in range(n)]
+                    gains = [gain[h, t:t + 8, :] for t in tops]
+                for i in range(n):
+                    parts = []
+                    for u in range(2):
+                        acc = None
+                        for j in range(n):
+                            term = held[j * n + i if inverse else i * n + j] * xs[j][u]
+                            acc = term if acc is None else acc + term
+                        parts.append(acc if inverse else acc * gains[u])
+                    rows = jnp.concatenate(parts, axis=0).astype(jnp.bfloat16)
+                    if inverse:
+                        top = (first + i) * chan + q * G
+                        msgs[top:top + G, pl.ds(at, lanes)] = rows
+                    else:
+                        top = PLACE[first + i] * chan + q * G
+                        turned[top:top + G, cols] = rows
+
+            for q in range(chan // G):
+                steps.append(functools.partial(go, q, off, first, n, held))
+        return steps
+
+    def mixing():
+        for lo, hi, w in ((3, 7, wide_one), (0, 3, wide_zero), (7, 9, wide_two)):
+            mixed[lo * chan:hi * chan, :] = jnp.dot(
+                w[...], turned[lo * chan:hi * chan, :], preferred_element_type=jnp.float32)
+
+    for h in range(2):
+        weave(gather(0, h))
+        weave(turn(0, h))
 
     def block(b, _):
-        base = pl.multiple_of(b * EDGE_BLOCK, EDGE_BLOCK)
-        take_rows(lambda i: src[i], base, EDGE_BLOCK)
-        wscr[0:35, :] = wig[:, pl.ds(base, EDGE_BLOCK)]
-        wt = wscr[...].T
-        for k in range(35):
-            spread[k] = jnp.broadcast_to(wt[:, k:k + 1], (EDGE_BLOCK, chan))
-        for q in range(EDGE_BLOCK // G):
-            rows = slice(q * G, (q + 1) * G)
-            rr = rad[pl.ds(base + q * G, G), :].astype(jnp.float32)
-            xs = [stage[pl.ds(q * G * ROWS + c, G, stride=ROWS), :] for c in range(ROWS)]
-            for off, first, n in BLOCKS:
-                for i in range(n):
-                    acc = None
-                    for j in range(n):
-                        term = spread[off + i * n + j, rows, :] * xs[first + j]
-                        acc = term if acc is None else acc + term
-                    at = PLACE[first + i] * chan
-                    turned[rows, at:at + chan] = (acc * rr).astype(jnp.bfloat16)
-        mixed[:, 0:3 * chan] = jnp.dot(turned[:, 0:3 * chan], w_zero[...], preferred_element_type=jnp.float32)
-        mixed[:, 3 * chan:7 * chan] = jnp.dot(
-            turned[:, 3 * chan:7 * chan], pair_one[...], preferred_element_type=jnp.float32)
-        mixed[:, 7 * chan:] = jnp.dot(turned[:, 7 * chan:], pair_two[...], preferred_element_type=jnp.float32)
-        for q in range(EDGE_BLOCK // G):
-            rows = slice(q * G, (q + 1) * G)
-            xs = [mixed[rows, PLACE[c] * chan:(PLACE[c] + 1) * chan] for c in range(ROWS)]
-            for off, first, n in BLOCKS:
-                for i in range(n):
-                    acc = None
-                    for j in range(n):
-                        term = spread[off + j * n + i, rows, :] * xs[first + j]
-                        acc = term if acc is None else acc + term
-                    c = first + i
-                    msgs[c // 2, pl.ds(base + q * G, G), (c % 2) * chan:(c % 2 + 1) * chan] = (
-                        acc.astype(jnp.bfloat16))
-        return 0
-
-    lax.fori_loop(0, edges // EDGE_BLOCK, block, 0)
+        base = pl.multiple_of(b * width, width)
+        after = pl.multiple_of(jnp.where(b + 1 < n_block, b + 1, 0) * width, width)
+        weave(rotate(base, 0, False), gather(after, 0))
+        weave(rotate(base, 1, False), gather(after, 1), turn(after, 0))
+        mixing()
+        weave(rotate(base, 0, True) + rotate(base, 1, True), turn(after, 1))
+        return 0
+
+    lax.fori_loop(0, n_block, block, 0)
 
     def hand_over(p, w):
         return pltpu.make_async_remote_copy(
             src_ref=sums.at[p, :, pl.ds(0, w)], dst_ref=arrived.at[p, :, pl.ds(0, w)],
             send_sem=s_send.at[p], recv_sem=s_recv.at[p], device_id=(s, mate), device_id_type=MESH)
 
+    def total_of(lo, hi, p, w):
+        return lax.dot_general(
+            onehot[lo:hi, :], msgs[p * 2 * chan:p * 2 * chan + w, :], (((1,), (1,)), ((), ())),
+            preferred_element_type=jnp.float32)
+
     widths = [2 * chan] * 4 + [chan]
     for p, w in enumerate(widths):
-        sums[p, :, 0:w] = jnp.dot(onehot[0:half, :], msgs[p, :, 0:w], preferred_element_type=jnp.float32)
+        sums[p, :, 0:w] = total_of(0, half, p, w)
         hand_over(p, w).start()
     for p, w in enumerate(widths):
-        own = jnp.dot(onehot[half:, :], msgs[p, :, 0:w], preferred_element_type=jnp.float32)
+        own = total_of(half, 2 * half, p, w)
         hand_over(p, w).wait()
         total = ((own + arrived[p, :, 0:w]) * message_scale).astype(jnp.bfloat16)
         out[2 * p] = total[:, 0:chan]
@@ -221,13 +276,14 @@
             pltpu.VMEM((face // 2 * rows, chan), jnp.bfloat16),
             pltpu.VMEM((face * rows, chan), jnp.bfloat16),
             pltpu.VMEM((face * rows, chan), jnp.bfloat16),
-            pltpu.VMEM((EDGE_BLOCK * rows, chan), jnp.float32),
-            pltpu.VMEM((128, EDGE_BLOCK), jnp.float32),
-            pltpu.VMEM((35, EDGE_BLOCK, chan), jnp.float32),
-            pltpu.VMEM((EDGE_BLOCK, rows * chan), jnp.bfloat16),
-            pltpu.VMEM((EDGE_BLOCK, rows * chan), jnp.float32),
-            pltpu.VMEM((5, edges, 2 * chan), jnp.bfloat16),
+            pltpu.VMEM((2, 128 * rows, chan), jnp.float32),
+            pltpu.VMEM((2, rows, chan, 128), jnp.float32),
+            pltpu.VMEM((2, chan, 128), jnp.float32),
+            pltpu.VMEM((rows * chan, 256), jnp.bfloat16),
+            pltpu.VMEM((rows * chan, 256), jnp.float32),
+            pltpu.VMEM((rows * chan, edges), jnp.bfloat16),
             pltpu.VMEM((atoms, edges), jnp.bfloat16),
+            pltpu.VMEM((3 * chan, 3 * chan), jnp.bfloat16),
             pltpu.VMEM((4 * chan, 4 * chan), jnp.bfloat16),
             pltpu.VMEM((2 * chan, 2 * chan), jnp.bfloat16),
             pltpu.VMEM((5, half, 2 * chan), jnp.float32),
@@ -240,7 +296,7 @@
         compiler_params=pltpu.CompilerParams(
             collective_id=0, has_side_effects=True, vmem_limit_bytes=62 * 1024 * 1024),
         name="layer",
-    )(boundary[0], sources, block_counts, jnp.transpose(nodes, (1, 0, 2)), targets[None, :],
+    )(boundary[0], sources, block_counts.T, jnp.transpose(nodes, (1, 0, 2)), targets,
       wigner, radial, w_zero, w_one, w_two)
     return jnp.transpose(out, (1, 0, 2))
 

time: 85.2 us -> 68.2 us (0.80)
  Pallas kernels: 79.9 us -> 65.7 us
  local copies, waits for them, and re-layouts: 5.08 us -> 2.36 us
    pallas_call x1, Pallas kernels: 79.9 us -> 65.7 us  [per_device(): pl.pallas_call(layer_kernel, out_shape=jax.ShapeDtypeStruct((rows, half,...]
    unnamed x2 -> x1, local copies, waits for them, and re-layouts: 3.77 us -> 2.36 us
    broadcast_in_dim x1 -> x0, local copies, waits for them, and re-layouts: 1.31 us -> none  [per_device(): targets[None, :]]
where the time goes in v2:
time: 68.2 us; the launch traced here: 68.1 us
  Pallas kernels  65.7 us (96%)
  local copies, waits for them, and re-layouts  2.36 us (3%)
    pallas_call x1, Pallas kernels, per_device(): pl.pallas_call(layer_kernel, out_shape=jax.ShapeDtypeStruct((rows, half,...  65.7 us
    unnamed x1, local copies, waits for them, and re-layouts  2.36 us

profile of v2, /device:TPU:1, one launch (start us, length us, event | category | flops | bytes accessed | tf_op | source)
XLA Modules:
  0.0 68.1 jit_solution(9757194089268731358)
XLA Ops:
  0.0 65.7 %layer.1 = bf16[9,512,128]{2,1,0:T(8,128)(2,1)} custom-call(s32[2,640]{1,0:T(2,128)} %bitcast.6, s32[2560]{0:T(1024)} %src.1, s32[2,128]{1,0:T(2,128)} %bitcast.7, bf16[9,512,128]{2,1,0:T(8,128)(2,1)} %bitcast.5, s32[2560]{0:T(1024)} %tgt.1, f32[35,2560]{1,0:T(8,128)} %wig.1, bf16[2560,128]{1,0:T(8,128)(2,1)} %rad.1, bf16[384,384]{1,0:T(8,128)(2,1)} %w_zero.1, ...), custom_call_target="tpu_custom_call" | custom-call | tf_op jit(solution)/shard_map/layer/pallas_call | solution.py:267
  65.7 2.4 %copy.12 = bf16[512,9,128]{2,0,1:T(8,128)(2,1)} copy(bf16[512,9,128]{2,0,1:T(8,128)(2,1)} %bitcast.4) | data formatting | bytes 2359296

commit v3 on v2

--- a/solution.py
+++ b/solution.py
@@ -13,7 +13,7 @@
 PLACE = {0: 0, 2: 1, 6: 2, 3: 3, 7: 4, 1: 5, 5: 6, 8: 7, 4: 8}
 MESH = pl.DeviceIdType.MESH
 message_scale = 0.2
-CHUNK = 64
+CHUNK = 32
 
 
 def weave(*lists):
@@ -23,9 +23,10 @@
 
 
 def layer_kernel(
-    boundary, src, counts, nodes, tgt, wig, rad, w_zero, w_one, w_two, out,
-    table, other, send_up, send_down, from_below, from_above, stage, across, gain,
-    turned, mixed, msgs, onehot, wide_zero, wide_one, wide_two, sums, arrived,
+    boundary_hbm, src_hbm, counts_hbm, nodes_hbm, tgt_hbm, wig_hbm, rad_hbm, zero_hbm, one_hbm, two_hbm, out,
+    boundary, src, counts, nodes, tgt, wig, rad, w_zero, w_one, w_two, local_sem,
+    table, other, send_up, send_down, from_below, from_above, stage, across, gain, spread,
+    turned, mixed, msgs, onehot, goal, wide_zero, wide_one, wide_two, sums, leaving, arrived,
     n_send, n_recv, up_send, up_recv, down_send, down_recv,
     fb_send, fb_recv, fa_send, fa_recv, s_send, s_recv,
 ):
@@ -44,13 +45,21 @@
     n_chunk = mine // CHUNK
     crows = CHUNK * ROWS
 
+    local = [
+        pltpu.make_async_copy(a, b, local_sem.at[i])
+        for i, (a, b) in enumerate((
+            (nodes_hbm, nodes), (boundary_hbm, boundary), (zero_hbm, w_zero), (one_hbm, w_one), (two_hbm, w_two),
+            (counts_hbm, counts), (tgt_hbm, tgt), (src_hbm, src), (wig_hbm, wig), (rad_hbm, rad)))]
+    for copy in local:
+        copy.start()
+
     barrier = pltpu.get_barrier_semaphore()
     for where in ((s, mate), (up, g), (down, g)):
         pl.semaphore_signal(barrier, inc=1, device_id=where, device_id_type=MESH)
     pl.semaphore_wait(barrier, 3)
 
     swap = pltpu.make_async_remote_copy(
-        src_ref=nodes, dst_ref=other, send_sem=n_send, recv_sem=n_recv,
+        src_ref=nodes_hbm, dst_ref=other, send_sem=n_send, recv_sem=n_recv,
         device_id=(s, mate), device_id_type=MESH)
     swap.start()
 
@@ -63,7 +72,10 @@
             return 0
         lax.fori_loop(0, half // 16, step, 0, unroll=2)
 
+    local[0].wait()
     fill(nodes, g * half)
+    for copy in local[1:5]:
+        copy.wait()
 
     width = w_one.shape[1]
     wide_zero[...] = w_zero[...].T
@@ -107,18 +119,31 @@
 
     lax.fori_loop(0, n_chunk, send_face, 0)
 
+    for copy in local[5:]:
+        copy.wait()
+
     live = counts[g, s] * EDGE_BLOCK
     slot = lax.broadcasted_iota(jnp.int32, (1, edges), 1)
-    goal = jnp.where(slot < live, tgt[...].reshape(1, edges), -1)
+    goal[...] = jnp.where(slot < live, tgt[...].reshape(1, edges), -1)
+    atom = lax.broadcasted_iota(jnp.int32, (128, half), 1)
 
     def mark(i, _):
-        at = pl.multiple_of(i * 16, 16)
-        first = jnp.where(at < half, mate * half + at, g * half + at - half)
-        atom = first + lax.broadcasted_iota(jnp.int32, (16, edges), 0)
-        onehot[pl.ds(at, 16), :] = jnp.where(atom == goal, 1.0, 0.0).astype(jnp.bfloat16)
-        return 0
-
-    lax.fori_loop(0, slab_atoms // 16, mark, 0)
+        at = pl.multiple_of(i * 128, 128)
+        aim = jnp.broadcast_to(goal[:, pl.ds(at, 128)], (128, 128)).T
+        aim = jnp.concatenate([aim] * (half // 128), axis=1)
+        for k, who in enumerate((mate, g)):
+            onehot[k, pl.ds(at, 128), :] = jnp.where(aim == atom + who * half, 1.0, 0.0).astype(jnp.bfloat16)
+        return 0
+
+    lax.fori_loop(0, edges // 128, mark, 0)
+
+    def clear(i, _):
+        for k in range(2):
+            sums[k, pl.ds(pl.multiple_of(i * 32, 32), 32), :] = jnp.zeros((32, half), jnp.float32)
+        return 0
+
+    lax.fori_loop(0, ROWS * chan // 32, clear, 0)
+    msgs[:, edges - 512:] = jnp.zeros((ROWS * chan, 512), jnp.bfloat16)
 
     def forward(k, buf, ss, rs):
         part = buf.at[pl.ds(pl.multiple_of((g * n_chunk + k) * crows, crows), crows), :]
@@ -151,7 +176,7 @@
 
     lax.fori_loop(0, n_chunk, finish_land, 0)
 
-    G = 16
+    G = 32
     lanes = 128
     width = 2 * lanes
     n_block = edges // width
@@ -171,21 +196,20 @@
             gain[h] = rad[pl.ds(base + h * lanes, lanes), :].astype(jnp.float32).T
         return [one(c) for c in range(ROWS)] + [radial]
 
-    def wide(k, at):
-        return jnp.broadcast_to(wig[k:k + 1, pl.ds(at, lanes)], (8, lanes))
+    def widen_rows(base, h):
+        def go():
+            for k in range(wig.shape[0]):
+                spread[h, k] = jnp.broadcast_to(wig[k:k + 1, pl.ds(base + h * lanes, lanes)], (8, lanes))
+        return [go]
 
     def rotate(base, h, inverse):
         at = base + h * lanes
         cols = slice(h * lanes, (h + 1) * lanes)
         steps = []
         for off, first, n in BLOCKS:
-            held = {}
-
-            def go(q, off, first, n, held):
-                if q == 0:
-                    for k in range(n * n):
-                        held[k] = wide(off + k, at)
-                tops = (q * G, q * G + 8)
+
+            def go(q, off, first, n):
+                tops = range(q * G, (q + 1) * G, 8)
                 if inverse:
                     xs = [[mixed[PLACE[first + j] * chan + t:PLACE[first + j] * chan + t + 8, cols] for t in tops]
                           for j in range(n)]
@@ -194,10 +218,10 @@
                     gains = [gain[h, t:t + 8, :] for t in tops]
                 for i in range(n):
                     parts = []
-                    for u in range(2):
+                    for u in range(len(tops)):
                         acc = None
                         for j in range(n):
-                            term = held[j * n + i if inverse else i * n + j] * xs[j][u]
+                            term = spread[h, off + (j * n + i if inverse else i * n + j)] * xs[j][u]
                             acc = term if acc is None else acc + term
                         parts.append(acc if inverse else acc * gains[u])
                     rows = jnp.concatenate(parts, axis=0).astype(jnp.bfloat16)
@@ -209,7 +233,7 @@
                         turned[top:top + G, cols] = rows
 
             for q in range(chan // G):
-                steps.append(functools.partial(go, q, off, first, n, held))
+                steps.append(functools.partial(go, q, off, first, n))
         return steps
 
     def mixing():
@@ -221,38 +245,55 @@
         weave(gather(0, h))
         weave(turn(0, h))
 
+    span = 2 * width
+
+    def add_up(side, pair):
+        cols = pl.ds(pl.multiple_of(pair * span, span), span)
+
+        def one(p):
+            def go():
+                atoms = slice(p * 256, (p + 1) * 256)
+                sums[side, :, atoms] += jnp.dot(
+                    msgs[:, cols], onehot[side, cols, atoms], preferred_element_type=jnp.float32)
+            return go
+        return [one(p) for p in range(half // 256)]
+
     def block(b, _):
         base = pl.multiple_of(b * width, width)
+        pair = jnp.where(b < 2, n_block // 2 - 1, b // 2 - 1)
+        adds = add_up(lax.rem(b, 2), pair)
         after = pl.multiple_of(jnp.where(b + 1 < n_block, b + 1, 0) * width, width)
-        weave(rotate(base, 0, False), gather(after, 0))
-        weave(rotate(base, 1, False), gather(after, 1), turn(after, 0))
+        weave(widen_rows(base, 0))
+        weave(widen_rows(base, 1))
+        weave(rotate(base, 0, False), gather(after, 0), adds[0:1])
+        weave(rotate(base, 1, False), gather(after, 1), turn(after, 0), adds[1:2])
         mixing()
-        weave(rotate(base, 0, True) + rotate(base, 1, True), turn(after, 1))
+        weave(turn(after, 1))
+        weave(rotate(base, 0, True))
+        weave(rotate(base, 1, True))
         return 0
 
     lax.fori_loop(0, n_block, block, 0)
 
-    def hand_over(p, w):
+    part = 3 * chan
+
+    def hand_over(p):
         return pltpu.make_async_remote_copy(
-            src_ref=sums.at[p, :, pl.ds(0, w)], dst_ref=arrived.at[p, :, pl.ds(0, w)],
+            src_ref=leaving.at[p], dst_ref=arrived.at[p],
             send_sem=s_send.at[p], recv_sem=s_recv.at[p], device_id=(s, mate), device_id_type=MESH)
 
-    def total_of(lo, hi, p, w):
-        return lax.dot_general(
-            onehot[lo:hi, :], msgs[p * 2 * chan:p * 2 * chan + w, :], (((1,), (1,)), ((), ())),
-            preferred_element_type=jnp.float32)
-
-    widths = [2 * chan] * 4 + [chan]
-    for p, w in enumerate(widths):
-        sums[p, :, 0:w] = total_of(0, half, p, w)
-        hand_over(p, w).start()
-    for p, w in enumerate(widths):
-        own = total_of(half, 2 * half, p, w)
-        hand_over(p, w).wait()
-        total = ((own + arrived[p, :, 0:w]) * message_scale).astype(jnp.bfloat16)
-        out[2 * p] = total[:, 0:chan]
-        if w > chan:
-            out[2 * p + 1] = total[:, chan:]
+    last = n_block // 2 - 1
+    weave(add_up(0, last))
+    for p in range(3):
+        leaving[p] = sums[0, p * part:(p + 1) * part, :].astype(jnp.bfloat16)
+        hand_over(p).start()
+    weave(add_up(1, last))
+    for p in range(3):
+        hand_over(p).wait()
+        total = sums[1, p * part:(p + 1) * part, :] + arrived[p].astype(jnp.float32)
+        total = (total * message_scale).astype(jnp.bfloat16)
+        for c in range(3):
+            out[3 * p + c] = total[c * chan:(c + 1) * chan, :].T
 
 
 def per_device(nodes, boundary, sources, targets, block_counts, wigner, radial, w_zero, w_one, w_two):
@@ -262,14 +303,25 @@
     n_chunk = face // 2 // CHUNK
     atoms = 2 * half
     vm = pl.BlockSpec(memory_space=pltpu.VMEM)
-    sm = pl.BlockSpec(memory_space=pltpu.SMEM)
+    hbm = pl.BlockSpec(memory_space=pltpu.HBM)
     dma = pltpu.SemaphoreType.DMA
     out = pl.pallas_call(
         layer_kernel,
         out_shape=jax.ShapeDtypeStruct((rows, half, chan), jnp.bfloat16),
-        in_specs=[sm, sm, sm] + [vm] * 7,
+        in_specs=[hbm] * 10,
         out_specs=vm,
         scratch_shapes=[
+            pltpu.SMEM((2, face), jnp.int32),
+            pltpu.SMEM((edges,), jnp.int32),
+            pltpu.SMEM(block_counts.shape[::-1], jnp.int32),
+            pltpu.VMEM((rows, half, chan), jnp.bfloat16),
+            pltpu.VMEM((edges,), jnp.int32),
+            pltpu.VMEM(wigner.shape, jnp.float32),
+            pltpu.VMEM(radial.shape, jnp.bfloat16),
+            pltpu.VMEM(w_zero.shape, jnp.bfloat16),
+            pltpu.VMEM(w_one.shape, jnp.bfloat16),
+            pltpu.VMEM(w_two.shape, jnp.bfloat16),
+            dma((10,)),
             pltpu.VMEM(((atoms + 2 * face) * rows, chan), jnp.float32),
             pltpu.VMEM((rows, half, chan), jnp.bfloat16),
             pltpu.VMEM((face // 2 * rows, chan), jnp.bfloat16),
@@ -279,19 +331,22 @@
             pltpu.VMEM((2, 128 * rows, chan), jnp.float32),
             pltpu.VMEM((2, rows, chan, 128), jnp.float32),
             pltpu.VMEM((2, chan, 128), jnp.float32),
+            pltpu.VMEM((2, 35, 8, 128), jnp.float32),
             pltpu.VMEM((rows * chan, 256), jnp.bfloat16),
             pltpu.VMEM((rows * chan, 256), jnp.float32),
             pltpu.VMEM((rows * chan, edges), jnp.bfloat16),
-            pltpu.VMEM((atoms, edges), jnp.bfloat16),
+            pltpu.VMEM((2, edges, half), jnp.bfloat16),
+            pltpu.VMEM((1, edges), jnp.int32),
             pltpu.VMEM((3 * chan, 3 * chan), jnp.bfloat16),
             pltpu.VMEM((4 * chan, 4 * chan), jnp.bfloat16),
             pltpu.VMEM((2 * chan, 2 * chan), jnp.bfloat16),
-            pltpu.VMEM((5, half, 2 * chan), jnp.float32),
-            pltpu.VMEM((5, half, 2 * chan), jnp.float32),
+            pltpu.VMEM((2, rows * chan, half), jnp.float32),
+            pltpu.VMEM((3, 3 * chan, half), jnp.bfloat16),
+            pltpu.VMEM((3, 3 * chan, half), jnp.bfloat16),
             dma, dma,
             dma((n_chunk,)), dma((n_chunk,)), dma((n_chunk,)), dma((n_chunk,)),
             dma((n_chunk,)), dma((n_chunk,)), dma((n_chunk,)), dma((n_chunk,)),
-            dma((5,)), dma((5,)),
+            dma((3,)), dma((3,)),
         ],
         compiler_params=pltpu.CompilerParams(
             collective_id=0, has_side_effects=True, vmem_limit_bytes=62 * 1024 * 1024),

time: 68.2 us -> 60.6 us (0.89)
  Pallas kernels: 65.7 us -> 58.1 us
    pallas_call x1, Pallas kernels: 65.7 us -> 58.1 us  [per_device(): pl.pallas_call(layer_kernel, out_shape=jax.ShapeDtypeStruct((rows, half,...]
where the time goes in v3:
time: 60.6 us; the launch traced here: 60.4 us
  Pallas kernels  58.1 us (96%)
  local copies, waits for them, and re-layouts  2.36 us (4%)
    pallas_call x1, Pallas kernels, per_device(): pl.pallas_call(layer_kernel, out_shape=jax.ShapeDtypeStruct((rows, half,...  58.1 us
    unnamed x1, local copies, waits for them, and re-layouts  2.36 us

profile of v3, /device:TPU:1, one launch (start us, length us, event | category | flops | bytes accessed | tf_op | source)
XLA Modules:
  0.0 60.4 jit_solution(13029550219046935325)
XLA Ops:
  0.0 58.1 %layer.1 = bf16[9,512,128]{2,1,0:T(8,128)(2,1)} custom-call(s32[2,640]{1,0:T(2,128)} %bitcast.6, s32[2560]{0:T(1024)} %src_hbm.1, s32[2,128]{1,0:T(2,128)} %bitcast.7, bf16[9,512,128]{2,1,0:T(8,128)(2,1)} %bitcast.5, s32[2560]{0:T(1024)} %tgt_hbm.1, f32[35,2560]{1,0:T(8,128)} %wig_hbm.1, bf16[2560,128]{1,0:T(8,128)(2,1)} %rad_hbm.1, ...), custom_call_target="tpu_custom_call" | custom-call | tf_op jit(solution)/shard_map/layer/pallas_call | solution.py:308
  58.1 2.4 %copy.12 = bf16[512,9,128]{2,0,1:T(8,128)(2,1)} copy(bf16[512,9,128]{2,0,1:T(8,128)(2,1)} %bitcast.4) | data formatting | bytes 2359296

commit v4 on v3

--- a/solution.py
+++ b/solution.py
@@ -159,6 +159,12 @@
         (send_down, from_above, down_send, down_recv, down, fa_send, fa_recv, (slab_atoms + face) * ROWS),
     )
 
+    def finish_land(k, _):
+        for buf, dst, ss, rs, to, fs, fr, base in sides:
+            forward(k, dst, fs, fr).wait()
+            widen(dst, (mate * n_chunk + k) * crows, base)
+        return 0
+
     def land(k, _):
         for buf, dst, ss, rs, to, fs, fr, base in sides:
             face_copy(k, buf, dst, ss, rs, to).wait()
@@ -166,15 +172,13 @@
             widen(dst, (g * n_chunk + k) * crows, base)
         return 0
 
-    lax.fori_loop(0, n_chunk, land, 0)
-
-    def finish_land(k, _):
-        for buf, dst, ss, rs, to, fs, fr, base in sides:
-            forward(k, dst, fs, fr).wait()
-            widen(dst, (mate * n_chunk + k) * crows, base)
-        return 0
-
-    lax.fori_loop(0, n_chunk, finish_land, 0)
+    def land_both(k, _):
+        land(k, 0)
+        return finish_land(k - 1, 0)
+
+    land(0, 0)
+    lax.fori_loop(1, n_chunk, land_both, 0)
+    finish_land(n_chunk - 1, 0)
 
     G = 32
     lanes = 128
@@ -349,10 +353,11 @@
             dma((3,)), dma((3,)),
         ],
         compiler_params=pltpu.CompilerParams(
-            collective_id=0, has_side_effects=True, vmem_limit_bytes=62 * 1024 * 1024),
+            collective_id=0, has_side_effects=True, vmem_limit_bytes=48 * 1024 * 1024),
         name="layer",
-    )(boundary[0], sources, block_counts.T, jnp.transpose(nodes, (1, 0, 2)), targets,
-      wigner, radial, w_zero, w_one, w_two)
+    )(*[pltpu.with_memory_space_constraint(a, pltpu.HBM) for a in (
+        boundary[0], sources, block_counts.T, jnp.transpose(nodes, (1, 0, 2)), targets,
+        wigner, radial, w_zero, w_one, w_two)])
     return jnp.transpose(out, (1, 0, 2))
 
 

time: 60.6 us -> 58.1 us (0.959)
  local copies, waits for them, and re-layouts: 2.36 us -> 1.02 us
  Pallas kernels: 58.1 us -> 57 us
    unnamed x1, local copies, waits for them, and re-layouts: 2.36 us -> 1.02 us
    pallas_call x1, Pallas kernels: 58.1 us -> 57 us  [per_device(): pl.pallas_call(layer_kernel, out_shape=jax.ShapeDtypeStruct((rows, half,...]
where the time goes in v4:
time: 58.1 us
  Pallas kernels  57 us (98%)
  local copies, waits for them, and re-layouts  1.02 us (2%)
    pallas_call x1, Pallas kernels, per_device(): pl.pallas_call(layer_kernel, out_shape=jax.ShapeDtypeStruct((rows, half,...  57 us

profile of v4, /device:TPU:1, one launch (start us, length us, event | category | flops | bytes accessed | tf_op | source)
XLA Modules:
  0.0 58.1 jit_solution(3780922989513333320)
XLA Ops:
  0.0 57.0 %layer.1 = bf16[9,512,128]{2,1,0:T(8,128)(2,1)S(1)} custom-call(s32[2,640]{1,0:T(2,128)} %bitcast.6, s32[2560]{0:T(1024)} %src_hbm.1, s32[2,128]{1,0:T(2,128)} %bitcast.7, bf16[9,512,128]{2,1,0:T(8,128)(2,1)} %bitcast.5, s32[2560]{0:T(1024)} %tgt_hbm.1, f32[35,2560]{1,0:T(8,128)} %wig_hbm.1, bf16[2560,128]{1,0:T(8,128)(2,1)} %rad_hbm.1, ...), custom_call_target="tpu_custom_call" | custom-call | tf_op jit(solution)/shard_map/layer/pallas_call | solution.py:312
  57.0 1.0 %copy.12 = bf16[512,9,128]{2,0,1:T(8,128)(2,1)} copy(bf16[512,9,128]{2,0,1:T(8,128)(2,1)S(1)} %bitcast.4) | data formatting | bytes 2359296

commit v5 on v4

--- a/solution.py
+++ b/solution.py
@@ -58,22 +58,25 @@
         pl.semaphore_signal(barrier, inc=1, device_id=where, device_id_type=MESH)
     pl.semaphore_wait(barrier, 3)
 
-    swap = pltpu.make_async_remote_copy(
-        src_ref=nodes_hbm, dst_ref=other, send_sem=n_send, recv_sem=n_recv,
-        device_id=(s, mate), device_id_type=MESH)
-    swap.start()
-
-    def fill(planes, first):
+    swaps = [
+        pltpu.make_async_remote_copy(
+            src_ref=nodes_hbm.at[pl.ds(3 * i, 3)], dst_ref=other.at[pl.ds(3 * i, 3)],
+            send_sem=n_send.at[i], recv_sem=n_recv.at[i], device_id=(s, mate), device_id_type=MESH)
+        for i in range(3)]
+    for swap in swaps:
+        swap.start()
+
+    def fill(planes, first, chosen):
         def step(i, _):
             at = pl.multiple_of(i * 16, 16)
-            for c in range(ROWS):
+            for c in chosen:
                 table[pl.ds((first + at) * ROWS + c, 16, stride=ROWS), :] = (
                     planes[c, pl.ds(at, 16), :].astype(jnp.float32))
             return 0
         lax.fori_loop(0, half // 16, step, 0, unroll=2)
 
     local[0].wait()
-    fill(nodes, g * half)
+    fill(nodes, g * half, range(ROWS))
     for copy in local[1:5]:
         copy.wait()
 
@@ -90,8 +93,9 @@
     wide_two[chan:, 0:chan] = imag
     wide_two[chan:, chan:] = real
 
-    swap.wait()
-    fill(other, mate * half)
+    for i, swap in enumerate(swaps):
+        swap.wait()
+        fill(other, mate * half, range(3 * i, 3 * i + 3))
 
     def take_row(row, h, i):
         r = row * ROWS
@@ -193,7 +197,7 @@
     def turn(base, h):
         def one(c):
             def go():
-                across[h, c] = stage[h, pl.ds(c, lanes, stride=ROWS), :].T
+                across[h, c] = stage[h, pl.ds(c, lanes, stride=ROWS), :].astype(jnp.bfloat16).T.astype(jnp.float32)
             return go
 
         def radial():
@@ -249,10 +253,8 @@
         weave(gather(0, h))
         weave(turn(0, h))
 
-    span = 2 * width
-
-    def add_up(side, pair):
-        cols = pl.ds(pl.multiple_of(pair * span, span), span)
+    def add_up(side, at):
+        cols = pl.ds(pl.multiple_of(at, width), width)
 
         def one(p):
             def go():
@@ -264,13 +266,13 @@
 
     def block(b, _):
         base = pl.multiple_of(b * width, width)
-        pair = jnp.where(b < 2, n_block // 2 - 1, b // 2 - 1)
-        adds = add_up(lax.rem(b, 2), pair)
+        done = jnp.where(b < 1, n_block - 1, b - 1) * width
+        adds = add_up(0, done) + add_up(1, done)
         after = pl.multiple_of(jnp.where(b + 1 < n_block, b + 1, 0) * width, width)
         weave(widen_rows(base, 0))
         weave(widen_rows(base, 1))
-        weave(rotate(base, 0, False), gather(after, 0), adds[0:1])
-        weave(rotate(base, 1, False), gather(after, 1), turn(after, 0), adds[1:2])
+        weave(rotate(base, 0, False), gather(after, 0), adds[0:2])
+        weave(rotate(base, 1, False), gather(after, 1), turn(after, 0), adds[2:4])
         mixing()
         weave(turn(after, 1))
         weave(rotate(base, 0, True))
@@ -286,7 +288,7 @@
             src_ref=leaving.at[p], dst_ref=arrived.at[p],
             send_sem=s_send.at[p], recv_sem=s_recv.at[p], device_id=(s, mate), device_id_type=MESH)
 
-    last = n_block // 2 - 1
+    last = edges - width
     weave(add_up(0, last))
     for p in range(3):
         leaving[p] = sums[0, p * part:(p + 1) * part, :].astype(jnp.bfloat16)
@@ -347,7 +349,7 @@
             pltpu.VMEM((2, rows * chan, half), jnp.float32),
             pltpu.VMEM((3, 3 * chan, half), jnp.bfloat16),
             pltpu.VMEM((3, 3 * chan, half), jnp.bfloat16),
-            dma, dma,
+            dma((3,)), dma((3,)),
             dma((n_chunk,)), dma((n_chunk,)), dma((n_chunk,)), dma((n_chunk,)),
             dma((n_chunk,)), dma((n_chunk,)), dma((n_chunk,)), dma((n_chunk,)),
             dma((3,)), dma((3,)),

time: 58.1 us -> 57.8 us (level)
  no operation moved by 1% of the time
where the time goes in v5:
time: 57.8 us
  Pallas kernels  56.7 us (98%)
  local copies, waits for them, and re-layouts  1.02 us (2%)
    pallas_call x1, Pallas kernels, per_device(): pl.pallas_call(layer_kernel, out_shape=jax.ShapeDtypeStruct((rows, half,...  56.7 us

profile of v5, /device:TPU:1, one launch (start us, length us, event | category | flops | bytes accessed | tf_op | source)
XLA Modules:
  0.0 57.8 jit_solution(16844464015549757719)
XLA Ops:
  0.0 56.7 %layer.1 = bf16[9,512,128]{2,1,0:T(8,128)(2,1)S(1)} custom-call(s32[2,640]{1,0:T(2,128)} %bitcast.6, s32[2560]{0:T(1024)} %src_hbm.1, s32[2,128]{1,0:T(2,128)} %bitcast.7, bf16[9,512,128]{2,1,0:T(8,128)(2,1)} %bitcast.5, s32[2560]{0:T(1024)} %tgt_hbm.1, f32[35,2560]{1,0:T(8,128)} %wig_hbm.1, bf16[2560,128]{1,0:T(8,128)(2,1)} %rad_hbm.1, ...), custom_call_target="tpu_custom_call" | custom-call | tf_op jit(solution)/shard_map/layer/pallas_call | solution.py:314
  56.8 1.0 %copy.12 = bf16[512,9,128]{2,0,1:T(8,128)(2,1)} copy(bf16[512,9,128]{2,0,1:T(8,128)(2,1)S(1)} %bitcast.4) | data formatting | bytes 2359296
